TPU v7x, 32 devices: a whole 2x2x4 slice. The times are simulated.
32 devices in a mesh: row: 8 (over z, y), kk: 4 (over x, core).
Axes of the slice: x: 2, y: 2, z: 4, core: 2. Of those that a mesh axis runs over, the one named last changes fastest.
Arguments:
- left_blocks: bfloat16 [4096, 4096], P('row', 'kk'), may hold values from -6 to 6
- right_blocks: bfloat16 [4096, 1024], P('kk', 'row'), may hold values from -0.125 to 0.125
- left_mask: int32 [32, 32], P('row', 'kk'), may hold values 0 or 1
- right_mask: int32 [32, 8], P('kk', 'row'), may hold values 0 or 1
- out_mask: int32 [32, 8], P('row'), may hold values 0 or 1
Outputs:
- product_blocks: bfloat16 [4096, 1024], P(('row', 'kk'))
All inputs are finite; a program needn't handle non-finite values. No bound on the sum of `left_mask` or of `right_mask` or of `out_mask` on one device may be relied on, other than what follows from the above.
Results may differ from a plain program's by a relative error of at most 0.001.
Values may be sent and summed in bfloat16 or wider, within the bound.
A program may use at most 192 MiB of HBM per device.

v0:
```python
import jax
import jax.numpy as jnp
from jax import lax
from jax.sharding import PartitionSpec as P


def expand(mask, size):
    return jnp.repeat(jnp.repeat(mask, size, axis=0), size, axis=1)


def per_device(left_blocks, right_blocks, left_mask, right_mask, out_mask):
    block = left_blocks.shape[0] // left_mask.shape[0]
    left_used = left_blocks * expand(left_mask, block).astype(jnp.bfloat16)
    right_used = right_blocks * expand(right_mask, block).astype(jnp.bfloat16)
    share = left_used.shape[0] // lax.axis_size("kk")
    right_all = lax.all_gather(right_used, "row", axis=1, tiled=True)
    summed = lax.psum_scatter(
        jnp.dot(left_used, right_all, preferred_element_type=jnp.float32),
        "kk",
        scatter_dimension=0,
        tiled=True,
    )
    mask_rows = expand(out_mask, block).astype(jnp.float32)
    own_mask = lax.dynamic_slice_in_dim(mask_rows, lax.axis_index("kk") * share, share, 0)
    return (summed * own_mask).astype(jnp.bfloat16)


def solution(mesh):
    in_specs = (P("row", "kk"), P("kk", "row"), P("row", "kk"), P("kk", "row"), P("row", None))
    out_specs = P(("row", "kk"), None)
    return jax.shard_map(
        per_device, mesh=mesh, in_specs=in_specs, out_specs=out_specs, check_vma=False
    )
```

profile of v0, /device:TPU:0, one launch (start us, length us, event | category | flops | bytes accessed | tf_op | source)
XLA Modules:
  0.0 105.5 jit_solution(10613878520376923319)
XLA Ops:
  6.5 0.0 copy-start.1
  6.5 0.0 all-gather.2.cloned.1.call-start
  6.5 0.7 convert_bitcast_fusion
  7.3 0.1 broadcast_bitcast_fusion
  7.4 1.9 %broadcast_multiply_fusion = bf16[1024,128]{1,0:T(8,128)(2,1)} fusion(bf16[1024,128]{1,0:T(8,128)(2,1)} %param.6, bf16[1024]{0:T(1024)(128)(2,1)S(1)} %broadcast_bitcast_fusion), kind=kLoop, calls=%fused_computation.5 | loop fusion | flops 131072 | bytes 526336 | tf_op jit(solution)/shard_map/mul | solution.py:14
  9.2 0.0 all-gather.2.cloned.1.call-update
  9.2 0.0 reduce-scatter.2.cloned.1.call-start
  9.3 0.7 convert_element_type.36
  10.0 52.5 %all-gather.2.cloned.1.call-done = bf16[1024,1024]{1,0:T(8,128)(2,1)} async-done(((bf16[1024,128]{1,0:T(8,128)(2,1)}), bf16[1024,1024]{1,0:T(8,128)(2,1)}) %all-gather.2.cloned.1.call-update) | async-done | bytes 2097168 | tf_op jit(solution)/shard_map/all_gather | solution.py:16
  62.5 0.6 broadcast_in_dim.17
  63.1 0.0 copy-done.1
  63.1 4.2 %fusion = f32[512,1024]{1,0:T(8,128)} fusion(bf16[1024,1024]{1,0:T(8,128)(2,1)} %all-gather.2.cloned.1.call-done, bf16[512,1024]{1,0:T(8,128)(2,1)S(1)} %copy-done.1, bf16[64,8,8,128]{3,2,1,0:T(8,128)(2,1)S(1)} %bitcast.18), kind=kOutput, calls=%fused_computation.2 | convolution fusion | flops 1074266112 | bytes 6291456 | tf_op jit(solution)/shard_map/dot_general | solution.py:18
  67.3 0.0 copy-start
  67.3 0.0 reduce-scatter.2.cloned.1.call-update
  67.4 0.7 copy-done
  68.0 0.6 broadcast_in_dim.20
  68.6 0.5 copy.13
  69.1 27.7 %reduce-scatter.2.cloned.1.call-done = f32[128,1024]{1,0:T(8,128)} async-done(((f32[512,1024]{1,0:T(8,128)}), f32[128,1024]{1,0:T(8,128)}) %reduce-scatter.2.cloned.1.call-update) | async-done | bytes 524304 | tf_op jit(solution)/shard_map/reduce_scatter | solution.py:17
  96.8 1.8 %multiply_convert_fusion = bf16[128,1024]{1,0:T(8,128)(2,1)} fusion(f32[128,1024]{1,0:T(8,128)} %reduce-scatter.2.cloned.1.call-done, f32[512,1024]{1,0:T(8,128)S(1)} %bitcast.16, s32[]{:T(128)S(6)} %select_n.3), kind=kLoop, calls=%fused_computation.4 | loop fusion | flops 262144 | bytes 1310724 | tf_op jit(solution)/shard_map/convert_element_type | solution.py:25
  (3 shorter events, 0.0 us)
Async XLA Ops:
  6.5 56.6 %copy-start.1 = (bf16[512,1024]{1,0:T(8,128)(2,1)S(1)}, bf16[512,1024]{1,0:T(8,128)(2,1)}, u32[]{:S(2)}) copy-start(bf16[512,1024]{1,0:T(8,128)(2,1)} %param.5) | copy-start | bytes 3145732
  6.5 55.9 %all-gather.2.cloned.1.call-start = ((), (), s32[]{:S(2)}) async-start(), calls=%async_computation.1 | async-start | bytes 2359296 | tf_op jit(solution)/shard_map/all_gather | solution.py:16
  9.2 87.6 %reduce-scatter.2.cloned.1.call-start = ((), (), s32[]{:S(2)}) async-start(), calls=%async_computation.2 | async-start | bytes 2621440 | tf_op jit(solution)/shard_map/reduce_scatter | solution.py:17
  67.3 0.7 copy-start
Sparse Core Ops, SparseCore 0:
  9.4 53.0 all-gather.1
  67.5 29.3 reduce-scatter.1
where the time goes:
time: 106 us; the launch traced here: 105 us
  waiting for transfers between devices  80.3 us (76%)
  between operations  13.4 us (13%)
  other arithmetic  5.09 us (5%)
  matrix products  4.2 us (4%)
  local copies, waits for them, and re-layouts  2.44 us (2%)
    all_gather x1, waiting for transfers between devices, per_device(): right_all = lax.all_gather(right_used, 'row', axis=1, tiled=True)  52.5 us
    reduce_scatter x1, waiting for transfers between devices, per_device(): lax.psum_scatter(jnp.dot(left_used, right_all, preferred_element_type=jnp...  27.7 us
    dot_general x1, matrix products, per_device(): jnp.dot(left_used, right_all, preferred_element_type=jnp.float32)  4.2 us
  transfers between devices with their start and end apart: 2, of which 2 were waited for; matrix products, arithmetic and copies ran while one was open for 2% of the time, Pallas kernels for 0%

commit v1 on v0

--- a/solution.py
+++ b/solution.py
@@ -2,6 +2,17 @@
 import jax.numpy as jnp
 from jax import lax
 from jax.sharding import PartitionSpec as P
+
+
+def turned_line(x, axis, along):
+    size = lax.axis_size(axis)
+    hops = [(i, (i + 1) % size) for i in range(size)]
+    terms = [x]
+    for far in range(1, size):
+        terms = [lax.ppermute(terms[0], axis, hops), *terms]
+    whole = jnp.concatenate(terms, axis=along)
+    shift = (lax.axis_index(axis) + 1) * terms[-1].shape[along]
+    return jnp.roll(whole, shift, axis=along)
 
 
 def expand(mask, size):
@@ -13,7 +24,7 @@
     left_used = left_blocks * expand(left_mask, block).astype(jnp.bfloat16)
     right_used = right_blocks * expand(right_mask, block).astype(jnp.bfloat16)
     share = left_used.shape[0] // lax.axis_size("kk")
-    right_all = lax.all_gather(right_used, "row", axis=1, tiled=True)
+    right_all = turned_line(right_used, "row", 1)
     summed = lax.psum_scatter(
         jnp.dot(left_used, right_all, preferred_element_type=jnp.float32),
         "kk",

time: 106 us -> 120 us (1.13)
  waiting for transfers between devices: 80.3 us -> 92.3 us
  starting transfers between devices: 0.04 us -> 3.07 us
  matrix products: 4.2 us -> 2.62 us
    ppermute x0 -> x7, waiting for transfers between devices: none -> 65 us  [turned_line(): terms = [lax.ppermute(terms[0], axis, hops), *terms]]
    all_gather x1 -> x0, waiting for transfers between devices: 52.5 us -> none  [per_device(): right_all = lax.all_gather(right_used, 'row', axis=1, tiled=True)]
    ppermute x0 -> x7, starting transfers between devices: none -> 3.06 us  [turned_line(): terms = [lax.ppermute(terms[0], axis, hops), *terms]]
    dot_general x1, matrix products: 4.2 us -> 2.62 us  [per_device(): jnp.dot(left_used, right_all, preferred_element_type=jnp.float32)]
  transfers between devices with their start and end apart: 2 -> 8, of which waited for: 2 -> 8; matrix products, arithmetic and copies ran while one was open for 2% -> 1% of each run, Pallas kernels for 0% -> 0%
where the time goes in v1:
time: 120 us; the launch traced here: 119 us
  waiting for transfers between devices  92.3 us (77%)
  between operations  13.6 us (11%)
  other arithmetic  4.87 us (4%)
  starting transfers between devices  3.07 us (3%)
  local copies, waits for them, and re-layouts  2.98 us (2%)
  matrix products  2.62 us (2%)
    ppermute x7, waiting for transfers between devices, turned_line(): terms = [lax.ppermute(terms[0], axis, hops), *terms]  65 us
    reduce_scatter x1, waiting for transfers between devices, per_device(): lax.psum_scatter(jnp.dot(left_used, right_all, preferred_element_type=jnp...  27.3 us
    ppermute x7, starting transfers between devices, turned_line(): terms = [lax.ppermute(terms[0], axis, hops), *terms]  3.06 us
    dot_general x1, matrix products, per_device(): jnp.dot(left_used, right_all, preferred_element_type=jnp.float32)  2.62 us
  transfers between devices with their start and end apart: 8, of which 8 were waited for; matrix products, arithmetic and copies ran while one was open for 1% of the time, Pallas kernels for 0%

profile of v1, /device:TPU:0, one launch (start us, length us, event | category | flops | bytes accessed | tf_op | source)
XLA Modules:
  0.0 119.5 jit_solution(14429798386551561590)
XLA Ops:
  6.5 0.7 convert_bitcast_fusion
  7.3 1.1 broadcast_multiply_fusion
  8.5 3.0 %collective-permute-start = (bf16[1024,128]{1,0:T(8,128)(2,1)S(1)}, bf16[1024,128]{1,0:T(8,128)(2,1)S(1)}, u32[]{:S(2)}, u32[]{:S(2)}) collective-permute-start(bf16[1024,128]{1,0:T(8,128)(2,1)S(1)} %broadcast_multiply_fusion), channel_id=1, source_target_pairs={{0,4},{4,8},{8,12},{12,16},{16,20},{20,24},{24,28},{28,0},{1,5},{5... | collective-permute-start | bytes 786440 | tf_op jit(solution)/shard_map/ppermute | solution.py:12
  11.5 9.3 %collective-permute-done = bf16[1024,128]{1,0:T(8,128)(2,1)S(1)} collective-permute-done((bf16[1024,128]{1,0:T(8,128)(2,1)S(1)}, bf16[1024,128]{1,0:T(8,128)(2,1)S(1)}, u32[]{:S(2)}, u32[]{:S(2)}) %collective-permute-start) | collective-permute-done | bytes 262176 | tf_op jit(solution)/shard_map/ppermute | solution.py:12
  20.9 10.2 %collective-permute-done.1 = bf16[1024,128]{1,0:T(8,128)(2,1)S(1)} collective-permute-done((bf16[1024,128]{1,0:T(8,128)(2,1)S(1)}, bf16[1024,128]{1,0:T(8,128)(2,1)S(1)}, u32[]{:S(2)}, u32[]{:S(2)}) %collective-permute-start.1) | collective-permute-done | bytes 262176 | tf_op jit(solution)/shard_map/ppermute | solution.py:12
  31.0 9.3 %collective-permute-done.2 = bf16[1024,128]{1,0:T(8,128)(2,1)S(1)} collective-permute-done((bf16[1024,128]{1,0:T(8,128)(2,1)S(1)}, bf16[1024,128]{1,0:T(8,128)(2,1)S(1)}, u32[]{:S(2)}, u32[]{:S(2)}) %collective-permute-start.2) | collective-permute-done | bytes 262176 | tf_op jit(solution)/shard_map/ppermute | solution.py:12
  40.3 9.1 %collective-permute-done.3 = bf16[1024,128]{1,0:T(8,128)(2,1)S(1)} collective-permute-done((bf16[1024,128]{1,0:T(8,128)(2,1)S(1)}, bf16[1024,128]{1,0:T(8,128)(2,1)S(1)}, u32[]{:S(2)}, u32[]{:S(2)}) %collective-permute-start.3) | collective-permute-done | bytes 262176 | tf_op jit(solution)/shard_map/ppermute | solution.py:12
  49.4 9.1 %collective-permute-done.4 = bf16[1024,128]{1,0:T(8,128)(2,1)S(1)} collective-permute-done((bf16[1024,128]{1,0:T(8,128)(2,1)S(1)}, bf16[1024,128]{1,0:T(8,128)(2,1)S(1)}, u32[]{:S(2)}, u32[]{:S(2)}) %collective-permute-start.4) | collective-permute-done | bytes 262176 | tf_op jit(solution)/shard_map/ppermute | solution.py:12
  58.5 9.7 %collective-permute-done.5 = bf16[1024,128]{1,0:T(8,128)(2,1)S(1)} collective-permute-done((bf16[1024,128]{1,0:T(8,128)(2,1)S(1)}, bf16[1024,128]{1,0:T(8,128)(2,1)S(1)}, u32[]{:S(2)}, u32[]{:S(2)}) %collective-permute-start.5) | collective-permute-done | bytes 262176 | tf_op jit(solution)/shard_map/ppermute | solution.py:12
  68.2 0.7 convert_element_type.36
  68.8 8.4 %collective-permute-done.6 = bf16[1024,128]{1,0:T(8,128)(2,1)S(1)} collective-permute-done((bf16[1024,128]{1,0:T(8,128)(2,1)S(1)}, bf16[1024,128]{1,0:T(8,128)(2,1)S(1)}, u32[]{:S(2)}, u32[]{:S(2)}) %collective-permute-start.6) | collective-permute-done | bytes 262176 | tf_op jit(solution)/shard_map/ppermute | solution.py:12
  77.3 0.1 constant_dynamic-update-slice_fusion.14
  77.4 0.1 constant_dynamic-update-slice_fusion.13
  77.6 0.1 constant_dynamic-update-slice_fusion.11
  77.8 0.1 constant_dynamic-update-slice_fusion.9
  77.9 0.3 constant_dynamic-update-slice_fusion.8
  78.2 0.1 constant_dynamic-update-slice_fusion.6
  78.8 0.3 constant_dynamic-update-slice_fusion
  79.1 0.6 broadcast_in_dim.17
  79.7 2.6 %fusion = f32[512,1024]{1,0:T(8,128)} fusion(bf16[1024,2048]{1,0:T(8,128)(2,1)S(1)} %constant_dynamic-update-slice_fusion, s32[]{:T(128)S(6)} %select_n.17, bf16[512,1024]{1,0:T(8,128)(2,1)S(1)} %copy-done.2, bf16[64,8,8,128]{3,2,1,0:T(8,128)(2,1)S(1)} %bitcast.17), kind=kOutput, calls=%fused_computation.1 | convolution fusion | flops 1074266112 | bytes 6291460 | tf_op jit(solution)/shard_map/dot_general | solution.py:29
  82.4 0.6 broadcast_in_dim.20
  83.0 0.5 copy.13
  83.5 27.3 %reduce-scatter.2.cloned.1.call-done = f32[128,1024]{1,0:T(8,128)} async-done(((f32[512,1024]{1,0:T(8,128)}), f32[128,1024]{1,0:T(8,128)}) %reduce-scatter.2.cloned.1.call-update) | async-done | bytes 524304 | tf_op jit(solution)/shard_map/reduce_scatter | solution.py:28
  110.8 1.8 %multiply_convert_fusion = bf16[128,1024]{1,0:T(8,128)(2,1)} fusion(f32[128,1024]{1,0:T(8,128)} %reduce-scatter.2.cloned.1.call-done, f32[512,1024]{1,0:T(8,128)S(1)} %bitcast.15, s32[]{:T(128)S(6)} %select_n.18), kind=kLoop, calls=%fused_computation.5 | loop fusion | flops 262144 | bytes 1310724 | tf_op jit(solution)/shard_map/convert_element_type | solution.py:36
  (27 shorter events, 0.9 us)
Async XLA Ops:
  6.5 71.3 %copy-start = (bf16[1024,128]{1,0:T(8,128)(2,1)S(1)}, bf16[1024,128]{1,0:T(8,128)(2,1)}, u32[]{:S(2)}) copy-start(bf16[1024,128]{1,0:T(8,128)(2,1)} %param.6) | copy-start | bytes 786436
  6.5 104.3 %reduce-scatter.2.cloned.1.call-start = ((), (), s32[]{:S(2)}) async-start(), calls=%async_computation.1 | async-start | bytes 2621440 | tf_op jit(solution)/shard_map/reduce_scatter | solution.py:28
  8.5 12.4 %collective-permute-start = (bf16[1024,128]{1,0:T(8,128)(2,1)S(1)}, bf16[1024,128]{1,0:T(8,128)(2,1)S(1)}, u32[]{:S(2)}, u32[]{:S(2)}) collective-permute-start(bf16[1024,128]{1,0:T(8,128)(2,1)S(1)} %broadcast_multiply_fusion), channel_id=1, source_target_pairs={{0,4},{4,8},{8,12},{12,16},{16,20},{20,24},{24,28},{28,0},{1,5},{5... | collective-permute-start | bytes 786440 | tf_op jit(solution)/shard_map/ppermute | solution.py:12
  20.9 10.2 %collective-permute-start.1 = (bf16[1024,128]{1,0:T(8,128)(2,1)S(1)}, bf16[1024,128]{1,0:T(8,128)(2,1)S(1)}, u32[]{:S(2)}, u32[]{:S(2)}) collective-permute-start(bf16[1024,128]{1,0:T(8,128)(2,1)S(1)} %collective-permute-done), channel_id=1, source_target_pairs={{0,4},{4,8},{8,12},{12,16},{16,20},{20,24},{24,28},{28,0},{1,5},{5... | collective-permute-start | bytes 786440 | tf_op jit(solution)/shard_map/ppermute | solution.py:12
  31.0 9.3 %collective-permute-start.2 = (bf16[1024,128]{1,0:T(8,128)(2,1)S(1)}, bf16[1024,128]{1,0:T(8,128)(2,1)S(1)}, u32[]{:S(2)}, u32[]{:S(2)}) collective-permute-start(bf16[1024,128]{1,0:T(8,128)(2,1)S(1)} %collective-permute-done.1), channel_id=1, source_target_pairs={{0,4},{4,8},{8,12},{12,16},{16,20},{20,24},{24,28},{28,0},{1,5},{5... | collective-permute-start | bytes 786440 | tf_op jit(solution)/shard_map/ppermute | solution.py:12
  40.3 9.1 %collective-permute-start.3 = (bf16[1024,128]{1,0:T(8,128)(2,1)S(1)}, bf16[1024,128]{1,0:T(8,128)(2,1)S(1)}, u32[]{:S(2)}, u32[]{:S(2)}) collective-permute-start(bf16[1024,128]{1,0:T(8,128)(2,1)S(1)} %collective-permute-done.2), channel_id=1, source_target_pairs={{0,4},{4,8},{8,12},{12,16},{16,20},{20,24},{24,28},{28,0},{1,5},{5... | collective-permute-start | bytes 786440 | tf_op jit(solution)/shard_map/ppermute | solution.py:12
  49.4 9.1 %collective-permute-start.4 = (bf16[1024,128]{1,0:T(8,128)(2,1)S(1)}, bf16[1024,128]{1,0:T(8,128)(2,1)S(1)}, u32[]{:S(2)}, u32[]{:S(2)}) collective-permute-start(bf16[1024,128]{1,0:T(8,128)(2,1)S(1)} %collective-permute-done.3), channel_id=1, source_target_pairs={{0,4},{4,8},{8,12},{12,16},{16,20},{20,24},{24,28},{28,0},{1,5},{5... | collective-permute-start | bytes 786440 | tf_op jit(solution)/shard_map/ppermute | solution.py:12
  58.5 9.7 %collective-permute-start.5 = (bf16[1024,128]{1,0:T(8,128)(2,1)S(1)}, bf16[1024,128]{1,0:T(8,128)(2,1)S(1)}, u32[]{:S(2)}, u32[]{:S(2)}) collective-permute-start(bf16[1024,128]{1,0:T(8,128)(2,1)S(1)} %collective-permute-done.4), channel_id=1, source_target_pairs={{0,4},{4,8},{8,12},{12,16},{16,20},{20,24},{24,28},{28,0},{1,5},{5... | collective-permute-start | bytes 786440 | tf_op jit(solution)/shard_map/ppermute | solution.py:12
  68.2 9.1 %collective-permute-start.6 = (bf16[1024,128]{1,0:T(8,128)(2,1)S(1)}, bf16[1024,128]{1,0:T(8,128)(2,1)S(1)}, u32[]{:S(2)}, u32[]{:S(2)}) collective-permute-start(bf16[1024,128]{1,0:T(8,128)(2,1)S(1)} %collective-permute-done.5), channel_id=1, source_target_pairs={{0,4},{4,8},{8,12},{12,16},{16,20},{20,24},{24,28},{28,0},{1,5},{5... | collective-permute-start | bytes 786440 | tf_op jit(solution)/shard_map/ppermute | solution.py:12
  77.5 2.2 %copy-start.2 = (bf16[512,1024]{1,0:T(8,128)(2,1)S(1)}, bf16[512,1024]{1,0:T(8,128)(2,1)}, u32[]{:S(2)}) copy-start(bf16[512,1024]{1,0:T(8,128)(2,1)} %param.5) | copy-start | bytes 3145732
  79.7 2.7 %copy-start.1 = (s32[4,8]{1,0:T(4,128)S(1)}, s32[4,8]{1,0:T(4,128)}, u32[]{:S(2)}) copy-start(s32[4,8]{1,0:T(4,128)} %param.9) | copy-start | bytes 388
Sparse Core Ops, SparseCore 0:
  82.5 28.2 reduce-scatter.1
